TPU v7x, 32 devices: a whole 2x2x4 slice. The times are simulated.
32 devices in a mesh: branch: 2 (over x), seq: 16 (over z, y, core).
Axes of the slice: x: 2, y: 2, z: 4, core: 2. Of those that a mesh axis runs over, the one named last changes fastest.
Arguments:
- queries: bfloat16 [8192, 2048], P(('branch', 'seq')), parts along dimension 0, may hold values from -8 to 8
- keys: bfloat16 [8192, 2048], P(('branch', 'seq')), parts along dimension 0, may hold values from -8 to 8
- values: bfloat16 [8192, 2048], P(('branch', 'seq')), parts along dimension 0, may hold values from -6 to 6
- out_grad: bfloat16 [8192, 2048], P(('branch', 'seq')), parts along dimension 0, may hold values from -6 to 6
- segments: int32 [8192], P(('branch', 'seq')), parts along dimension 0, may hold values from 0 to 7, never falling along the last dimension, each value on 1 to 768 neighbouring positions
Outputs:
- attended: bfloat16 [8192, 2048], P(('branch', 'seq')), parts along dimension 0
- query_grad: bfloat16 [8192, 2048], P(('branch', 'seq')), parts along dimension 0
- key_grad: bfloat16 [8192, 2048], P(('branch', 'seq')), parts along dimension 0
- value_grad: bfloat16 [8192, 2048], P(('branch', 'seq')), parts along dimension 0
There are 2 independent parts, one for each index of `branch`. A program takes and returns all parts, laid end to end along the dimension named above; each array names one. Nothing has to cross between parts.
Inputs may be any that keep to these rules, and one draw needn't show every extreme that they name: `segments`: never falling along the sequence; each document has 1 to 768 tokens, and one has exactly 768.
All inputs are finite; a program needn't handle non-finite values.
Results may differ from a plain program's by a relative error of at most 0.017.
Values may be sent and summed in bfloat16 or wider, within the bound.
A program may use at most 128 MiB of HBM per device.

v0:
```python
import functools
import math

import jax
import jax.numpy as jnp
from jax import lax
from jax.experimental import pallas as pl
from jax.experimental.pallas import tpu as pltpu
from jax.sharding import PartitionSpec as P

HEADS = 16
REACH = 3
TAIL = 4
MESH = pl.DeviceIdType.MESH
HIDDEN = -1e30
NT = (((1,), (1,)), ((), ()))
NN = (((1,), (0,)), ((), ()))


def dot(a, b, dims):
    return lax.dot_general(a, b, dims, preferred_element_type=jnp.float32)


def kernel(
    count, rows, head_dim,
    q_in, k_in, v_in, g_in, seg_row, seg_col,
    o_out, dq_out, dk_out, dv_out,
    qb, kb, vb, gb, kseg, qseg, stat, bias, bias_t,
    send_sem, recv_sem, seg_send, seg_recv, stat_send, stat_recv,
):
    me = lax.axis_index("seq")
    odd = me % 2
    second = (me // 2) % 2
    partner = me + 1 - 2 * odd
    chunks = HEADS
    inv_root = 1.0 / math.sqrt(head_dim)
    log2_scale = inv_root * math.log2(math.e)
    bufs = (kb, vb, qb, gb)
    ins = (k_in, v_in, q_in, g_in)
    KV, QG = (0, 1), (2, 3)
    far = range(1, REACH + 1)

    def to(target):
        return {"seq": target}

    def columns(c):
        return pl.ds(pl.multiple_of(c * head_dim, head_dim), head_dim)

    def piece(t, slot, c):
        if isinstance(slot, int) and slot == 0:
            return ins[t].at[:, columns(c)]
        return bufs[t].at[slot, :, columns(c)]

    def load(t, slot, cols):
        return ins[t][:, cols] if slot == 0 else bufs[t][slot, :, cols]

    def send(ts, from_slot, to_slot, kind, c, target):
        for t in ts:
            pltpu.make_async_remote_copy(
                src_ref=piece(t, from_slot, c),
                dst_ref=piece(t, to_slot, c),
                send_sem=send_sem.at[t, kind, c],
                recv_sem=recv_sem.at[t, to_slot, c],
                device_id=to(target),
                device_id_type=MESH,
            ).start()

    def landed(ts, slot, c):
        for t in ts:
            pltpu.make_async_copy(piece(t, slot, c), piece(t, slot, c), recv_sem.at[t, slot, c]).wait()

    direct_up = me + 1 + 2 * odd
    direct_down = me - 3 + 2 * odd
    slot_up = 1 + 2 * odd
    slot_down = 3 - 2 * odd
    first = second == 0
    last = second == 1
    sends = {
        (KV, 0): first & (me + 2 < count),
        (QG, 0): last & (me - 2 >= 0),
        (KV, 1): direct_up < count,
        (QG, 1): direct_down >= 0,
        (KV, 2): me - 2 >= 0,
        (QG, 2): me + 2 < count,
        (KV, 3): last & (odd == 0) & (me + 5 < count),
        (QG, 3): first & (odd == 1) & (me - 5 >= 0),
        (KV, 4): last & (me >= 4),
        (QG, 4): first & (me + 4 < count),
    }

    barrier = pltpu.get_barrier_semaphore()
    met = 0
    for d in (1, 2, 3, 5):
        for peer, there in ((me + d, me + d < count), (me - d, me - d >= 0)):
            @pl.when(there)
            def _():
                pl.semaphore_signal(barrier, inc=1, device_id=to(peer), device_id_type=MESH)
            met = met + jnp.where(there, 1, 0)
    pl.semaphore_wait(barrier, met)

    def seg_copy(way, d, target):
        return pltpu.make_async_remote_copy(
            src_ref=seg_row,
            dst_ref=(kseg, qseg)[way].at[d],
            send_sem=seg_send.at[way, d],
            recv_sem=seg_recv.at[way, d],
            device_id=to(target),
            device_id_type=MESH,
        )

    def along_z(ts, c):
        slot, target = (slot_up, direct_up) if ts == KV else (slot_down, direct_down)

        @pl.when(sends[ts, 1])
        def _():
            send(ts, 0, slot, 1, c, target)

        @pl.when(sends[ts, 3])
        def _():
            send(ts, 0, 4, 3, c, me + 5 if ts == KV else me - 5)

    def own_y(ts, c):
        @pl.when(sends[ts, 0])
        def _():
            send(ts, 0, 2, 0, c, me + 2 if ts == KV else me - 2)

    def forward_y(ts, c):
        slot, target = (3 + odd, me - 1 - 2 * odd) if ts == KV else (4 - odd, me + 3 - 2 * odd)

        @pl.when(sends[ts, 4])
        def _():
            landed(ts, slot, c)
            send(ts, slot, 2, 4, c, target)

    def relay(ts, c):
        @pl.when(sends[ts, 2])
        def _():
            landed(ts, 2, c)
            send(ts, 2, slot_down if ts == KV else slot_up, 2, c, partner)

    for d in far:
        @pl.when(me + d < count)
        def _():
            seg_copy(0, d, me + d).start()

        @pl.when(me - d >= 0)
        def _():
            seg_copy(1, d, me - d).start()

    def start_keys(c, carry):
        own_y(KV, c)
        along_z(KV, c)
        return carry

    def start_queries(c, carry):
        along_z(QG, c)
        return carry

    lax.fori_loop(0, chunks, start_keys, 0)
    lax.fori_loop(0, chunks, start_queries, 0)

    for d in far:
        @pl.when(me - d < 0)
        def _():
            kb[d] = jnp.zeros(kb.shape[1:], kb.dtype)
            vb[d] = jnp.zeros(vb.shape[1:], vb.dtype)
            kseg[d] = jnp.full(kseg.shape[1:], -1, kseg.dtype)

        @pl.when(me + d >= count)
        def _():
            qb[d] = jnp.zeros(qb.shape[1:], qb.dtype)
            gb[d] = jnp.zeros(gb.shape[1:], gb.dtype)
            qseg[d] = jnp.full(qseg.shape[1:], -1, qseg.dtype)
            stat[d] = jnp.zeros(stat.shape[1:], stat.dtype)

    forward_y(KV, 0)
    own_col = jnp.broadcast_to(seg_col[...], (rows, rows))
    upper = lax.broadcasted_iota(jnp.int32, (rows, rows), 0)
    across = lax.broadcasted_iota(jnp.int32, (rows, rows), 1)
    same = own_col == seg_row[0:1, :]
    bias[0] = jnp.where(same & (across <= upper), 0.0, HIDDEN)
    bias_t[0] = jnp.where(same & (upper <= across), 0.0, HIDDEN)
    for d in far:
        @pl.when(me - d >= 0)
        def _():
            pltpu.make_async_copy(seg_row, kseg.at[d], seg_recv.at[0, d]).wait()

        @pl.when(me + d < count)
        def _():
            pltpu.make_async_copy(seg_row, qseg.at[d], seg_recv.at[1, d]).wait()
        bias[d] = jnp.where(own_col == kseg[d, 0:1, :], 0.0, HIDDEN)
        bias_t[d] = jnp.where(own_col == qseg[d, 0:1, :], 0.0, HIDDEN)
    relay(KV, 0)

    first_lane = lax.broadcasted_iota(jnp.int32, (rows, head_dim), 1) == 0
    span = range(REACH + 1)

    def own_queries(c):
        cols = columns(c)
        query = load(2, 0, cols)
        grad = load(3, 0, cols)
        scores = [dot(query, load(0, d, cols), NT) * log2_scale + bias[d] for d in span]
        peak = jnp.max(functools.reduce(jnp.maximum, scores), -1, keepdims=True)
        exponent = [jnp.exp2(s - peak) for s in scores]
        total = jnp.sum(functools.reduce(jnp.add, exponent), -1, keepdims=True)
        inverse = 1.0 / total
        weights = [(e * inverse).astype(jnp.bfloat16) for e in exponent]
        attended = functools.reduce(
            jnp.add, [dot(weights[d], load(1, d, cols), NN) for d in span]
        ).astype(jnp.bfloat16)
        o_out[:, cols] = attended
        delta = jnp.sum(grad.astype(jnp.float32) * attended.astype(jnp.float32), -1, keepdims=True)
        pair = jnp.where(first_lane, peak + jnp.log2(total), delta)
        stat[0, c] = pair.T[0:2]
        total_grad = None
        for d in span:
            dprob = dot(grad, load(1, d, cols), NT)
            dscore = (weights[d].astype(jnp.float32) * (dprob - delta)).astype(jnp.bfloat16)
            term = dot(dscore, load(0, d, cols), NN)
            total_grad = term if total_grad is None else total_grad + term
        dq_out[:, cols] = (total_grad * inv_root).astype(jnp.bfloat16)

    def own_keys(c):
        cols = columns(c)
        key = load(0, 0, cols)
        value = load(1, 0, cols)
        key_grad = value_grad = None
        for d in span:
            query = load(2, d, cols)
            grad = load(3, d, cols)
            lse = stat[d, c, 0:1, :]
            delta = stat[d, c, 1:2, :]
            scores = dot(key, query, NT) * log2_scale + bias_t[d]
            weights = jnp.exp2(scores - lse)
            dprob = dot(value, grad, NT)
            dscore = (weights * (dprob - delta)).astype(jnp.bfloat16)
            value_term = dot(weights.astype(jnp.bfloat16), grad, NN)
            key_term = dot(dscore, query, NN)
            value_grad = value_term if value_grad is None else value_grad + value_term
            key_grad = key_term if key_grad is None else key_grad + key_term
        dk_out[:, cols] = (key_grad * inv_root).astype(jnp.bfloat16)
        dv_out[:, cols] = value_grad.astype(jnp.bfloat16)

    def send_stats(c):
        for d in far:
            @pl.when(me - d >= 0)
            def _():
                pltpu.make_async_remote_copy(
                    src_ref=stat.at[0, c],
                    dst_ref=stat.at[d, c],
                    send_sem=stat_send.at[d, c],
                    recv_sem=stat_recv.at[d, c],
                    device_id=to(me - d),
                    device_id_type=MESH,
                ).start()

    def arrive_queries(c):
        @pl.when(me - 1 >= 0)
        def _():
            landed(KV, 1, c)

        @pl.when((me - 3 >= 0) & jnp.logical_not(last & (odd == 0)))
        def _():
            landed(KV, 3, c)

    def arrive_keys(c):
        @pl.when(me + 1 < count)
        def _():
            landed(QG, 1, c)

        @pl.when((me + 3 < count) & jnp.logical_not(first & (odd == 1)))
        def _():
            landed(QG, 3, c)
        for d in far:
            @pl.when(me + d < count)
            def _():
                pltpu.make_async_copy(stat.at[d, c], stat.at[d, c], stat_recv.at[d, c]).wait()

    def query_step(c, carry):
        @pl.when(c + 1 < chunks)
        def _():
            forward_y(KV, c + 1)
            relay(KV, c + 1)

        arrive_queries(c)
        own_queries(c)
        send_stats(c)
        forward_y(QG, c)

        @pl.when(c >= chunks - TAIL)
        def _():
            own_y(QG, c - (chunks - TAIL))
        return carry

    def key_step(c, carry):
        @pl.when(c + 1 < chunks)
        def _():
            relay(QG, c + 1)

        arrive_keys(c)
        own_keys(c)
        return carry

    def own_rest(c, carry):
        own_y(QG, c)
        return carry

    lax.fori_loop(0, chunks, query_step, 0)
    lax.fori_loop(TAIL, chunks, own_rest, 0)
    relay(QG, 0)
    lax.fori_loop(0, chunks, key_step, 0)

    def finish(c, carry):
        for (ts, kind), active in sends.items():
            @pl.when(active)
            def _():
                for t in ts:
                    pltpu.make_async_copy(piece(t, 0, c), piece(t, 0, c), send_sem.at[t, kind, c]).wait()
        for d in far:
            @pl.when(me - d >= 0)
            def _():
                pltpu.make_async_copy(stat.at[0, c], stat.at[0, c], stat_send.at[d, c]).wait()
        return carry

    lax.fori_loop(0, chunks, finish, 0)
    for d in far:
        @pl.when(me + d < count)
        def _():
            pltpu.make_async_copy(seg_row, seg_row, seg_send.at[0, d]).wait()

        @pl.when(me - d >= 0)
        def _():
            pltpu.make_async_copy(seg_row, seg_row, seg_send.at[1, d]).wait()


def solution(mesh):
    count = mesh.shape["seq"]

    def local(queries, keys, values, out_grad, segments):
        rows, feature = queries.shape
        head_dim = feature // HEADS
        seg_row = jnp.broadcast_to(segments[None, :], (8, rows))
        seg_col = segments[:, None]
        vmem = pl.BlockSpec(memory_space=pltpu.VMEM)
        slots = REACH + 1
        block = pltpu.VMEM((slots + 1, rows, feature), queries.dtype)
        seg_block = pltpu.VMEM((slots, 8, rows), jnp.int32)
        mask = pltpu.VMEM((slots, rows, rows), jnp.float32)
        dma = pltpu.SemaphoreType.DMA
        return pl.pallas_call(
            functools.partial(kernel, count, rows, head_dim),
            out_shape=[jax.ShapeDtypeStruct((rows, feature), jnp.bfloat16)] * 4,
            in_specs=[vmem] * 6,
            out_specs=[vmem] * 4,
            scratch_shapes=[block] * 4 + [
                seg_block, seg_block,
                pltpu.VMEM((slots, HEADS, 2, rows), jnp.float32),
                mask, mask,
                dma((4, 5, HEADS)), dma((4, slots + 1, HEADS)),
                dma((2, slots)), dma((2, slots)), dma((slots, HEADS)), dma((slots, HEADS)),
            ],
            compiler_params=pltpu.CompilerParams(
                collective_id=0, has_side_effects=True, vmem_limit_bytes=36 * 1024 * 1024
            ),
        )(queries, keys, values, out_grad, seg_row, seg_col)

    rows_spec = P(("branch", "seq"), None)
    return jax.shard_map(
        local,
        mesh=mesh,
        in_specs=(rows_spec,) * 4 + (P(("branch", "seq")),),
        out_specs=(rows_spec,) * 4,
        check_vma=False,
    )
```

profile of v0, /device:TPU:11, one launch (start us, length us, event | category | flops | bytes accessed | tf_op | source)
XLA Modules:
  0.0 120.8 jit_solution(4667718453184282569)
XLA Ops:
  0.6 0.0 copy-start.4
  0.6 0.7 copy-done.4
  1.3 0.1 copy.9.seg_col
  1.5 0.0 copy-start
  1.5 1.2 %copy-done = bf16[256,2048]{1,0:T(8,128)(2,1)S(1)} copy-done((bf16[256,2048]{1,0:T(8,128)(2,1)S(1)}, bf16[256,2048]{1,0:T(8,128)(2,1)}, u32[]{:S(2)}) %copy-start) | copy-done | bytes 1048600
  2.7 0.0 copy-start.1
  2.7 1.2 %copy-done.1 = bf16[256,2048]{1,0:T(8,128)(2,1)S(1)} copy-done((bf16[256,2048]{1,0:T(8,128)(2,1)S(1)}, bf16[256,2048]{1,0:T(8,128)(2,1)}, u32[]{:S(2)}) %copy-start.1) | copy-done | bytes 1048600
  3.9 0.0 copy-start.2
  3.9 1.2 %copy-done.2 = bf16[256,2048]{1,0:T(8,128)(2,1)S(1)} copy-done((bf16[256,2048]{1,0:T(8,128)(2,1)S(1)}, bf16[256,2048]{1,0:T(8,128)(2,1)}, u32[]{:S(2)}) %copy-start.2) | copy-done | bytes 1048600
  5.1 0.0 copy-start.3
  5.1 1.2 %copy-done.3 = bf16[256,2048]{1,0:T(8,128)(2,1)S(1)} copy-done((bf16[256,2048]{1,0:T(8,128)(2,1)S(1)}, bf16[256,2048]{1,0:T(8,128)(2,1)}, u32[]{:S(2)}) %copy-start.3) | copy-done | bytes 1048600
  6.4 110.6 %shard_map.84 = (bf16[256,2048]{1,0:T(8,128)(2,1)S(1)}, bf16[256,2048]{1,0:T(8,128)(2,1)S(1)}, bf16[256,2048]{1,0:T(8,128)(2,1)S(1)}, bf16[256,2048]{1,0:T(8,128)(2,1)S(1)}) custom-call(bf16[256,2048]{1,0:T(8,128)(2,1)S(1)} %copy-done, bf16[256,2048]{1,0:T(8,128)(2,1)S(1)} %copy-done.1, bf16[256,2048]{1,0:T(8,128)(2,1)S(1)} %copy-done.2, ...), custom_call_target="tpu_custom_call" | custom-call | tf_op jit(solution)/shard_map/pallas_call | solution.py:350
  116.9 1.0 copy.14
  117.9 1.0 copy.15
  118.9 1.0 copy.16
  119.8 1.0 copy.17
  (1 shorter events, 0.0 us)
Async XLA Ops:
  0.6 0.7 copy-start.4
  1.5 1.2 %copy-start = (bf16[256,2048]{1,0:T(8,128)(2,1)S(1)}, bf16[256,2048]{1,0:T(8,128)(2,1)}, u32[]{:S(2)}) copy-start(bf16[256,2048]{1,0:T(8,128)(2,1)} %q_in.1) | copy-start | bytes 3145732
  2.7 1.2 %copy-start.1 = (bf16[256,2048]{1,0:T(8,128)(2,1)S(1)}, bf16[256,2048]{1,0:T(8,128)(2,1)}, u32[]{:S(2)}) copy-start(bf16[256,2048]{1,0:T(8,128)(2,1)} %k_in.1) | copy-start | bytes 3145732
  3.9 1.2 %copy-start.2 = (bf16[256,2048]{1,0:T(8,128)(2,1)S(1)}, bf16[256,2048]{1,0:T(8,128)(2,1)}, u32[]{:S(2)}) copy-start(bf16[256,2048]{1,0:T(8,128)(2,1)} %v_in.1) | copy-start | bytes 3145732
  5.1 1.2 %copy-start.3 = (bf16[256,2048]{1,0:T(8,128)(2,1)S(1)}, bf16[256,2048]{1,0:T(8,128)(2,1)}, u32[]{:S(2)}) copy-start(bf16[256,2048]{1,0:T(8,128)(2,1)} %g_in.1) | copy-start | bytes 3145732
where the time goes:
time: 121 us
  Pallas kernels  111 us (92%)
  local copies, waits for them, and re-layouts  9.58 us (8%)
    pallas_call x1, Pallas kernels, local(): pl.pallas_call(functools.partial(kernel, count, rows, head_dim), out_shap...  111 us
    unnamed x14, local copies, waits for them, and re-layouts  9.45 us

commit v1 on v0

--- a/solution.py
+++ b/solution.py
@@ -10,7 +10,8 @@
 
 HEADS = 16
 REACH = 3
-TAIL = 4
+AHEAD = 4
+VMEM_LIMIT = 49 * 1024 * 1024
 MESH = pl.DeviceIdType.MESH
 HIDDEN = -1e30
 NT = (((1,), (1,)), ((), ()))
@@ -26,13 +27,15 @@
     q_in, k_in, v_in, g_in, seg_row, seg_col,
     o_out, dq_out, dk_out, dv_out,
     qb, kb, vb, gb, kseg, qseg, stat, bias, bias_t,
-    send_sem, recv_sem, seg_send, seg_recv, stat_send, stat_recv,
+    load_sem, send_sem, recv_sem, seg_send, seg_recv, stat_send, stat_recv,
 ):
     me = lax.axis_index("seq")
     odd = me % 2
     second = (me // 2) % 2
     partner = me + 1 - 2 * odd
     chunks = HEADS
+    pairs = count // 4
+    pair = me // 4
     inv_root = 1.0 / math.sqrt(head_dim)
     log2_scale = inv_root * math.log2(math.e)
     bufs = (kb, vb, qb, gb)
@@ -47,12 +50,10 @@
         return pl.ds(pl.multiple_of(c * head_dim, head_dim), head_dim)
 
     def piece(t, slot, c):
-        if isinstance(slot, int) and slot == 0:
-            return ins[t].at[:, columns(c)]
         return bufs[t].at[slot, :, columns(c)]
 
     def load(t, slot, cols):
-        return ins[t][:, cols] if slot == 0 else bufs[t][slot, :, cols]
+        return bufs[t][slot, :, cols]
 
     def send(ts, from_slot, to_slot, kind, c, target):
         for t in ts:
@@ -75,22 +76,46 @@
     slot_down = 3 - 2 * odd
     first = second == 0
     last = second == 1
-    sends = {
-        (KV, 0): first & (me + 2 < count),
-        (QG, 0): last & (me - 2 >= 0),
-        (KV, 1): direct_up < count,
-        (QG, 1): direct_down >= 0,
-        (KV, 2): me - 2 >= 0,
-        (QG, 2): me + 2 < count,
-        (KV, 3): last & (odd == 0) & (me + 5 < count),
-        (QG, 3): first & (odd == 1) & (me - 5 >= 0),
-        (KV, 4): last & (me >= 4),
-        (QG, 4): first & (me + 4 < count),
-    }
+    below = pair >= 1
+    above = pair + 1 < pairs
+
+    def share(c, amount):
+        return (c + 1) * amount // chunks > c * amount // chunks
+
+    def kv_near(row, c):
+        return share(c, chunks * (pairs - 1 - row) // pairs)
+
+    def qg_near(row, c):
+        return share(c, chunks * row // pairs)
+
+    def active(ts, kind, c):
+        if ts == KV:
+            return (
+                first & (me + 2 < count),
+                direct_up < count,
+                me - 2 >= 0,
+                last & (odd == 0) & above & jnp.logical_not(kv_near(pair, c)),
+                last & below & jnp.logical_not(kv_near(pair - 1, c)),
+                last & above & kv_near(pair, c),
+                first & above & kv_near(pair, c),
+            )[kind]
+        return (
+            last & (me - 2 >= 0),
+            direct_down >= 0,
+            me + 2 < count,
+            first & (odd == 1) & below & jnp.logical_not(qg_near(pair, c)),
+            first & above & jnp.logical_not(qg_near(pair + 1, c)),
+            first & below & qg_near(pair, c),
+            last & below & qg_near(pair, c),
+        )[kind]
+
+    loads = [pltpu.make_async_copy(ins[t], bufs[t].at[0], load_sem.at[t]) for t in range(4)]
+    for copy in loads:
+        copy.start()
 
     barrier = pltpu.get_barrier_semaphore()
     met = 0
-    for d in (1, 2, 3, 5):
+    for d in (1, 2, 3, 4, 5):
         for peer, there in ((me + d, me + d < count), (me - d, me - d >= 0)):
             @pl.when(there)
             def _():
@@ -108,32 +133,43 @@
             device_id_type=MESH,
         )
 
-    def along_z(ts, c):
+    def direct(ts, c):
         slot, target = (slot_up, direct_up) if ts == KV else (slot_down, direct_down)
 
-        @pl.when(sends[ts, 1])
+        @pl.when(active(ts, 1, c))
         def _():
             send(ts, 0, slot, 1, c, target)
 
-        @pl.when(sends[ts, 3])
+        @pl.when(active(ts, 3, c))
         def _():
             send(ts, 0, 4, 3, c, me + 5 if ts == KV else me - 5)
 
     def own_y(ts, c):
-        @pl.when(sends[ts, 0])
+        @pl.when(active(ts, 0, c))
         def _():
             send(ts, 0, 2, 0, c, me + 2 if ts == KV else me - 2)
 
-    def forward_y(ts, c):
+    def near_start(ts, c):
+        @pl.when(active(ts, 5, c))
+        def _():
+            send(ts, 0, 4, 5, c, me - 2 if ts == KV else me + 2)
+
+    def near_end(ts, c):
+        @pl.when(active(ts, 6, c))
+        def _():
+            landed(ts, 4, c)
+            send(ts, 4, 2, 6, c, me + 4 if ts == KV else me - 4)
+
+    def far_end(ts, c):
         slot, target = (3 + odd, me - 1 - 2 * odd) if ts == KV else (4 - odd, me + 3 - 2 * odd)
 
-        @pl.when(sends[ts, 4])
+        @pl.when(active(ts, 4, c))
         def _():
             landed(ts, slot, c)
             send(ts, slot, 2, 4, c, target)
 
     def relay(ts, c):
-        @pl.when(sends[ts, 2])
+        @pl.when(active(ts, 2, c))
         def _():
             landed(ts, 2, c)
             send(ts, 2, slot_down if ts == KV else slot_up, 2, c, partner)
@@ -149,14 +185,23 @@
 
     def start_keys(c, carry):
         own_y(KV, c)
-        along_z(KV, c)
+
+        @pl.when(c < AHEAD)
+        def _():
+            near_start(KV, c)
+
+        direct(KV, c)
         return carry
 
     def start_queries(c, carry):
-        along_z(QG, c)
-        return carry
-
+        direct(QG, c)
+        return carry
+
+    for copy in loads[:2]:
+        copy.wait()
     lax.fori_loop(0, chunks, start_keys, 0)
+    for copy in loads[2:]:
+        copy.wait()
     lax.fori_loop(0, chunks, start_queries, 0)
 
     for d in far:
@@ -173,7 +218,7 @@
             qseg[d] = jnp.full(qseg.shape[1:], -1, qseg.dtype)
             stat[d] = jnp.zeros(stat.shape[1:], stat.dtype)
 
-    forward_y(KV, 0)
+    far_end(KV, 0)
     own_col = jnp.broadcast_to(seg_col[...], (rows, rows))
     upper = lax.broadcasted_iota(jnp.int32, (rows, rows), 0)
     across = lax.broadcasted_iota(jnp.int32, (rows, rows), 1)
@@ -190,6 +235,7 @@
             pltpu.make_async_copy(seg_row, qseg.at[d], seg_recv.at[1, d]).wait()
         bias[d] = jnp.where(own_col == kseg[d, 0:1, :], 0.0, HIDDEN)
         bias_t[d] = jnp.where(own_col == qseg[d, 0:1, :], 0.0, HIDDEN)
+    near_end(KV, 0)
     relay(KV, 0)
 
     first_lane = lax.broadcasted_iota(jnp.int32, (rows, head_dim), 1) == 0
@@ -259,7 +305,7 @@
         def _():
             landed(KV, 1, c)
 
-        @pl.when((me - 3 >= 0) & jnp.logical_not(last & (odd == 0)))
+        @pl.when((me - 3 >= 0) & jnp.logical_not((odd == 0) & active(KV, 4, c)))
         def _():
             landed(KV, 3, c)
 
@@ -268,7 +314,7 @@
         def _():
             landed(QG, 1, c)
 
-        @pl.when((me + 3 < count) & jnp.logical_not(first & (odd == 1)))
+        @pl.when((me + 3 < count) & jnp.logical_not((odd == 1) & active(QG, 4, c)))
         def _():
             landed(QG, 3, c)
         for d in far:
@@ -277,24 +323,32 @@
                 pltpu.make_async_copy(stat.at[d, c], stat.at[d, c], stat_recv.at[d, c]).wait()
 
     def query_step(c, carry):
+        @pl.when(c + AHEAD < chunks)
+        def _():
+            near_start(KV, c + AHEAD)
+
         @pl.when(c + 1 < chunks)
         def _():
-            forward_y(KV, c + 1)
+            far_end(KV, c + 1)
+            near_end(KV, c + 1)
             relay(KV, c + 1)
+
+        near_start(QG, c)
+        far_end(QG, c)
+
+        @pl.when(c % pairs == 0)
+        def _():
+            own_y(QG, c // pairs)
 
         arrive_queries(c)
         own_queries(c)
         send_stats(c)
-        forward_y(QG, c)
-
-        @pl.when(c >= chunks - TAIL)
-        def _():
-            own_y(QG, c - (chunks - TAIL))
         return carry
 
     def key_step(c, carry):
         @pl.when(c + 1 < chunks)
         def _():
+            near_end(QG, c + 1)
             relay(QG, c + 1)
 
         arrive_keys(c)
@@ -306,16 +360,18 @@
         return carry
 
     lax.fori_loop(0, chunks, query_step, 0)
-    lax.fori_loop(TAIL, chunks, own_rest, 0)
+    lax.fori_loop(-(-chunks // pairs), chunks, own_rest, 0)
+    near_end(QG, 0)
     relay(QG, 0)
     lax.fori_loop(0, chunks, key_step, 0)
 
     def finish(c, carry):
-        for (ts, kind), active in sends.items():
-            @pl.when(active)
-            def _():
-                for t in ts:
-                    pltpu.make_async_copy(piece(t, 0, c), piece(t, 0, c), send_sem.at[t, kind, c]).wait()
+        for ts in (KV, QG):
+            for kind in range(7):
+                @pl.when(active(ts, kind, c))
+                def _():
+                    for t in ts:
+                        pltpu.make_async_copy(piece(t, 0, c), piece(t, 0, c), send_sem.at[t, kind, c]).wait()
         for d in far:
             @pl.when(me - d >= 0)
             def _():
@@ -350,17 +406,17 @@
         return pl.pallas_call(
             functools.partial(kernel, count, rows, head_dim),
             out_shape=[jax.ShapeDtypeStruct((rows, feature), jnp.bfloat16)] * 4,
-            in_specs=[vmem] * 6,
+            in_specs=[pl.BlockSpec(memory_space=pl.ANY)] * 4 + [vmem] * 2,
             out_specs=[vmem] * 4,
             scratch_shapes=[block] * 4 + [
                 seg_block, seg_block,
                 pltpu.VMEM((slots, HEADS, 2, rows), jnp.float32),
                 mask, mask,
-                dma((4, 5, HEADS)), dma((4, slots + 1, HEADS)),
+                dma((4,)), dma((4, 7, HEADS)), dma((4, slots + 1, HEADS)),
                 dma((2, slots)), dma((2, slots)), dma((slots, HEADS)), dma((slots, HEADS)),
             ],
             compiler_params=pltpu.CompilerParams(
-                collective_id=0, has_side_effects=True, vmem_limit_bytes=36 * 1024 * 1024
+                collective_id=0, has_side_effects=True, vmem_limit_bytes=VMEM_LIMIT
             ),
         )(queries, keys, values, out_grad, seg_row, seg_col)
 

time: 121 us -> 114 us (0.942)
  the two profiles are of different devices: /device:TPU:11 before, /device:TPU:7 now
where the time goes in v1:
time: 114 us
  Pallas kernels  109 us (96%)
  local copies, waits for them, and re-layouts  4.69 us (4%)
    pallas_call x1, Pallas kernels, local(): pl.pallas_call(functools.partial(kernel, count, rows, head_dim), out_shap...  109 us
    unnamed x6, local copies, waits for them, and re-layouts  4.55 us

profile of v1, /device:TPU:7, one launch (start us, length us, event | category | flops | bytes accessed | tf_op | source)
XLA Modules:
  0.0 114.0 jit_solution(13799514732270684316)
XLA Ops:
  0.6 0.0 copy-start
  0.6 0.7 copy-done
  1.3 0.1 copy.9.seg_col
  1.5 108.6 %shard_map.84 = (bf16[256,2048]{1,0:T(8,128)(2,1)S(1)}, bf16[256,2048]{1,0:T(8,128)(2,1)S(1)}, bf16[256,2048]{1,0:T(8,128)(2,1)S(1)}, bf16[256,2048]{1,0:T(8,128)(2,1)S(1)}) custom-call(bf16[256,2048]{1,0:T(8,128)(2,1)} %q_in.1, bf16[256,2048]{1,0:T(8,128)(2,1)} %k_in.1, bf16[256,2048]{1,0:T(8,128)(2,1)} %v_in.1, bf16[256,2048]{1,0:T(8,128)(2,1)} %g_in.1, ...), custom_call_target="tpu_custom_call" | custom-call | tf_op jit(solution)/shard_map/pallas_call | solution.py:406
  110.1 1.0 copy.14
  111.1 1.0 copy.15
  112.1 1.0 copy.16
  113.0 1.0 copy.17
  (1 shorter events, 0.0 us)
Async XLA Ops:
  0.6 0.7 copy-start

commit v2 on v1

--- a/solution.py
+++ b/solution.py
@@ -10,7 +10,7 @@
 
 HEADS = 16
 REACH = 3
-AHEAD = 4
+FILL = 6
 VMEM_LIMIT = 49 * 1024 * 1024
 MESH = pl.DeviceIdType.MESH
 HIDDEN = -1e30
@@ -79,14 +79,13 @@
     below = pair >= 1
     above = pair + 1 < pairs
 
-    def share(c, amount):
-        return (c + 1) * amount // chunks > c * amount // chunks
-
     def kv_near(row, c):
-        return share(c, chunks * (pairs - 1 - row) // pairs)
+        return c < chunks * (pairs - 1 - row) // pairs - 1
 
     def qg_near(row, c):
-        return share(c, chunks * row // pairs)
+        return c < (chunks - chunks // pairs) * row // pairs
+
+    paced = first & (odd == 1) & above & kv_near(pair, 0)
 
     def active(ts, kind, c):
         if ts == KV:
@@ -185,17 +184,36 @@
 
     def start_keys(c, carry):
         own_y(KV, c)
-
-        @pl.when(c < AHEAD)
-        def _():
-            near_start(KV, c)
-
+        near_start(KV, c)
+
+        @pl.when(jnp.logical_not(paced) | (c == 0))
+        def _():
+            direct(KV, c)
+        return carry
+
+    def start_queries(c, carry):
+        @pl.when(c < FILL)
+        def _():
+            own_y(QG, c)
+
+        direct(QG, c)
+        near_start(QG, c)
+        return carry
+
+    def direct_rest(c, carry):
         direct(KV, c)
         return carry
 
-    def start_queries(c, carry):
-        direct(QG, c)
-        return carry
+    def step_y(c):
+        far_end(KV, c)
+        near_end(KV, c)
+
+        @pl.when(paced)
+        def _():
+            stop = jnp.where(kv_near(pair, c + 1), c + 2, chunks)
+            lax.fori_loop(c + 1, jnp.where(kv_near(pair, c), stop, c + 1), direct_rest, 0)
+
+        relay(KV, c)
 
     for copy in loads[:2]:
         copy.wait()
@@ -218,7 +236,6 @@
             qseg[d] = jnp.full(qseg.shape[1:], -1, qseg.dtype)
             stat[d] = jnp.zeros(stat.shape[1:], stat.dtype)
 
-    far_end(KV, 0)
     own_col = jnp.broadcast_to(seg_col[...], (rows, rows))
     upper = lax.broadcasted_iota(jnp.int32, (rows, rows), 0)
     across = lax.broadcasted_iota(jnp.int32, (rows, rows), 1)
@@ -235,8 +252,7 @@
             pltpu.make_async_copy(seg_row, qseg.at[d], seg_recv.at[1, d]).wait()
         bias[d] = jnp.where(own_col == kseg[d, 0:1, :], 0.0, HIDDEN)
         bias_t[d] = jnp.where(own_col == qseg[d, 0:1, :], 0.0, HIDDEN)
-    near_end(KV, 0)
-    relay(KV, 0)
+    step_y(0)
 
     first_lane = lax.broadcasted_iota(jnp.int32, (rows, head_dim), 1) == 0
     span = range(REACH + 1)
@@ -322,23 +338,20 @@
             def _():
                 pltpu.make_async_copy(stat.at[d, c], stat.at[d, c], stat_recv.at[d, c]).wait()
 
+    def own_rest(c, carry):
+        own_y(QG, c)
+        return carry
+
     def query_step(c, carry):
-        @pl.when(c + AHEAD < chunks)
-        def _():
-            near_start(KV, c + AHEAD)
-
         @pl.when(c + 1 < chunks)
         def _():
-            far_end(KV, c + 1)
-            near_end(KV, c + 1)
-            relay(KV, c + 1)
-
-        near_start(QG, c)
+            step_y(c + 1)
+
         far_end(QG, c)
 
-        @pl.when(c % pairs == 0)
-        def _():
-            own_y(QG, c // pairs)
+        @pl.when(c + 2 == chunks)
+        def _():
+            lax.fori_loop(FILL, chunks, own_rest, 0)
 
         arrive_queries(c)
         own_queries(c)
@@ -355,12 +368,7 @@
         own_keys(c)
         return carry
 
-    def own_rest(c, carry):
-        own_y(QG, c)
-        return carry
-
     lax.fori_loop(0, chunks, query_step, 0)
-    lax.fori_loop(-(-chunks // pairs), chunks, own_rest, 0)
     near_end(QG, 0)
     relay(QG, 0)
     lax.fori_loop(0, chunks, key_step, 0)

time: 114 us -> 105 us (0.921)
  Pallas kernels: 109 us -> 99.5 us
    pallas_call x1, Pallas kernels: 109 us -> 99.5 us  [local(): pl.pallas_call(functools.partial(kernel, count, rows, head_dim), out_shap...]
where the time goes in v2:
time: 105 us
  Pallas kernels  99.5 us (95%)
  local copies, waits for them, and re-layouts  4.69 us (4%)
    pallas_call x1, Pallas kernels, local(): pl.pallas_call(functools.partial(kernel, count, rows, head_dim), out_shap...  99.5 us
    unnamed x6, local copies, waits for them, and re-layouts  4.55 us

profile of v2, /device:TPU:7, one launch (start us, length us, event | category | flops | bytes accessed | tf_op | source)
XLA Modules:
  0.0 104.8 jit_solution(13663410940014162194)
XLA Ops:
  0.6 0.0 copy-start
  0.6 0.7 copy-done
  1.3 0.1 copy.9.seg_col
  1.5 99.5 %shard_map.84 = (bf16[256,2048]{1,0:T(8,128)(2,1)S(1)}, bf16[256,2048]{1,0:T(8,128)(2,1)S(1)}, bf16[256,2048]{1,0:T(8,128)(2,1)S(1)}, bf16[256,2048]{1,0:T(8,128)(2,1)S(1)}) custom-call(bf16[256,2048]{1,0:T(8,128)(2,1)} %q_in.1, bf16[256,2048]{1,0:T(8,128)(2,1)} %k_in.1, bf16[256,2048]{1,0:T(8,128)(2,1)} %v_in.1, bf16[256,2048]{1,0:T(8,128)(2,1)} %g_in.1, ...), custom_call_target="tpu_custom_call" | custom-call | tf_op jit(solution)/shard_map/pallas_call | solution.py:414
  100.9 1.0 copy.14
  101.9 1.0 copy.15
  102.9 1.0 copy.16
  103.8 1.0 copy.17
  (1 shorter events, 0.0 us)
Async XLA Ops:
  0.6 0.7 copy-start

commit v3 on v2

--- a/solution.py
+++ b/solution.py
@@ -11,6 +11,8 @@
 HEADS = 16
 REACH = 3
 FILL = 6
+LAG = 4
+DRAIN_LIMIT = 48 * 1024 * 1024
 VMEM_LIMIT = 49 * 1024 * 1024
 MESH = pl.DeviceIdType.MESH
 HIDDEN = -1e30
@@ -24,9 +26,9 @@
 
 def kernel(
     count, rows, head_dim,
-    q_in, k_in, v_in, g_in, seg_row, seg_col,
+    q_in, k_in, v_in, g_in, seg_in,
     o_out, dq_out, dk_out, dv_out,
-    qb, kb, vb, gb, kseg, qseg, stat, bias, bias_t,
+    kvb, qgb, seg_row, kseg, qseg, stat, bias, bias_t,
     load_sem, send_sem, recv_sem, seg_send, seg_recv, stat_send, stat_recv,
 ):
     me = lax.axis_index("seq")
@@ -38,9 +40,9 @@
     pair = me // 4
     inv_root = 1.0 / math.sqrt(head_dim)
     log2_scale = inv_root * math.log2(math.e)
-    bufs = (kb, vb, qb, gb)
+    bufs = (kvb, qgb)
     ins = (k_in, v_in, q_in, g_in)
-    KV, QG = (0, 1), (2, 3)
+    KV, QG = 0, 1
     far = range(1, REACH + 1)
 
     def to(target):
@@ -49,26 +51,24 @@
     def columns(c):
         return pl.ds(pl.multiple_of(c * head_dim, head_dim), head_dim)
 
-    def piece(t, slot, c):
-        return bufs[t].at[slot, :, columns(c)]
+    def piece(ts, slot, c):
+        return bufs[ts].at[slot, :, :, columns(c)]
 
     def load(t, slot, cols):
-        return bufs[t][slot, :, cols]
+        return bufs[t // 2][slot, t % 2, :, cols]
 
     def send(ts, from_slot, to_slot, kind, c, target):
-        for t in ts:
-            pltpu.make_async_remote_copy(
-                src_ref=piece(t, from_slot, c),
-                dst_ref=piece(t, to_slot, c),
-                send_sem=send_sem.at[t, kind, c],
-                recv_sem=recv_sem.at[t, to_slot, c],
-                device_id=to(target),
-                device_id_type=MESH,
-            ).start()
+        pltpu.make_async_remote_copy(
+            src_ref=piece(ts, from_slot, c),
+            dst_ref=piece(ts, to_slot, c),
+            send_sem=send_sem.at[ts, kind, c],
+            recv_sem=recv_sem.at[ts, to_slot, c],
+            device_id=to(target),
+            device_id_type=MESH,
+        ).start()
 
     def landed(ts, slot, c):
-        for t in ts:
-            pltpu.make_async_copy(piece(t, slot, c), piece(t, slot, c), recv_sem.at[t, slot, c]).wait()
+        pltpu.make_async_copy(piece(ts, slot, c), piece(ts, slot, c), recv_sem.at[ts, slot, c]).wait()
 
     direct_up = me + 1 + 2 * odd
     direct_down = me - 3 + 2 * odd
@@ -108,7 +108,8 @@
             last & below & qg_near(pair, c),
         )[kind]
 
-    loads = [pltpu.make_async_copy(ins[t], bufs[t].at[0], load_sem.at[t]) for t in range(4)]
+    loads = [pltpu.make_async_copy(ins[t], bufs[t // 2].at[0, t % 2], load_sem.at[t]) for t in range(4)]
+    loads.append(pltpu.make_async_copy(seg_in, seg_row, load_sem.at[4]))
     for copy in loads:
         copy.start()
 
@@ -173,6 +174,7 @@
             landed(ts, 2, c)
             send(ts, 2, slot_down if ts == KV else slot_up, 2, c, partner)
 
+    loads[4].wait()
     for d in far:
         @pl.when(me + d < count)
         def _():
@@ -218,25 +220,23 @@
     for copy in loads[:2]:
         copy.wait()
     lax.fori_loop(0, chunks, start_keys, 0)
-    for copy in loads[2:]:
+    for copy in loads[2:4]:
         copy.wait()
     lax.fori_loop(0, chunks, start_queries, 0)
 
     for d in far:
         @pl.when(me - d < 0)
         def _():
-            kb[d] = jnp.zeros(kb.shape[1:], kb.dtype)
-            vb[d] = jnp.zeros(vb.shape[1:], vb.dtype)
+            kvb[d] = jnp.zeros(kvb.shape[1:], kvb.dtype)
             kseg[d] = jnp.full(kseg.shape[1:], -1, kseg.dtype)
 
         @pl.when(me + d >= count)
         def _():
-            qb[d] = jnp.zeros(qb.shape[1:], qb.dtype)
-            gb[d] = jnp.zeros(gb.shape[1:], gb.dtype)
+            qgb[d] = jnp.zeros(qgb.shape[1:], qgb.dtype)
             qseg[d] = jnp.full(qseg.shape[1:], -1, qseg.dtype)
             stat[d] = jnp.zeros(stat.shape[1:], stat.dtype)
 
-    own_col = jnp.broadcast_to(seg_col[...], (rows, rows))
+    own_col = jnp.broadcast_to(seg_row[0:1, :], (rows, rows)).T
     upper = lax.broadcasted_iota(jnp.int32, (rows, rows), 0)
     across = lax.broadcasted_iota(jnp.int32, (rows, rows), 1)
     same = own_col == seg_row[0:1, :]
@@ -358,11 +358,33 @@
         send_stats(c)
         return carry
 
+    def sent(ts, c):
+        for kind in range(7):
+            @pl.when(active(ts, kind, c))
+            def _():
+                pltpu.make_async_copy(piece(ts, 0, c), piece(ts, 0, c), send_sem.at[ts, kind, c]).wait()
+
+    def finish(c):
+        sent(KV, c)
+        sent(QG, c)
+        for d in far:
+            @pl.when(me - d >= 0)
+            def _():
+                pltpu.make_async_copy(stat.at[0, c], stat.at[0, c], stat_send.at[d, c]).wait()
+
+    def finish_rest(c, carry):
+        finish(c)
+        return carry
+
     def key_step(c, carry):
         @pl.when(c + 1 < chunks)
         def _():
             near_end(QG, c + 1)
             relay(QG, c + 1)
+
+        @pl.when(c >= LAG)
+        def _():
+            finish(c - LAG)
 
         arrive_keys(c)
         own_keys(c)
@@ -373,20 +395,7 @@
     relay(QG, 0)
     lax.fori_loop(0, chunks, key_step, 0)
 
-    def finish(c, carry):
-        for ts in (KV, QG):
-            for kind in range(7):
-                @pl.when(active(ts, kind, c))
-                def _():
-                    for t in ts:
-                        pltpu.make_async_copy(piece(t, 0, c), piece(t, 0, c), send_sem.at[t, kind, c]).wait()
-        for d in far:
-            @pl.when(me - d >= 0)
-            def _():
-                pltpu.make_async_copy(stat.at[0, c], stat.at[0, c], stat_send.at[d, c]).wait()
-        return carry
-
-    lax.fori_loop(0, chunks, finish, 0)
+    lax.fori_loop(chunks - LAG, chunks, finish_rest, 0)
     for d in far:
         @pl.when(me + d < count)
         def _():
@@ -395,6 +404,15 @@
         @pl.when(me - d >= 0)
         def _():
             pltpu.make_async_copy(seg_row, seg_row, seg_send.at[1, d]).wait()
+
+
+def drain(*refs):
+    ins, outs, sem = refs[:4], refs[4:8], refs[8]
+    copies = [pltpu.make_async_copy(ins[t], outs[t], sem.at[t]) for t in range(4)]
+    for copy in copies:
+        copy.start()
+    for copy in copies:
+        copy.wait()
 
 
 def solution(mesh):
@@ -403,30 +421,37 @@
     def local(queries, keys, values, out_grad, segments):
         rows, feature = queries.shape
         head_dim = feature // HEADS
-        seg_row = jnp.broadcast_to(segments[None, :], (8, rows))
-        seg_col = segments[:, None]
         vmem = pl.BlockSpec(memory_space=pltpu.VMEM)
         slots = REACH + 1
-        block = pltpu.VMEM((slots + 1, rows, feature), queries.dtype)
-        seg_block = pltpu.VMEM((slots, 8, rows), jnp.int32)
+        block = pltpu.VMEM((slots + 1, 2, rows, feature), queries.dtype)
+        seg_block = pltpu.VMEM((slots, 1, rows), jnp.int32)
         mask = pltpu.VMEM((slots, rows, rows), jnp.float32)
         dma = pltpu.SemaphoreType.DMA
-        return pl.pallas_call(
+        shapes = [jax.ShapeDtypeStruct((rows, feature), jnp.bfloat16)] * 4
+        results = pl.pallas_call(
             functools.partial(kernel, count, rows, head_dim),
-            out_shape=[jax.ShapeDtypeStruct((rows, feature), jnp.bfloat16)] * 4,
-            in_specs=[pl.BlockSpec(memory_space=pl.ANY)] * 4 + [vmem] * 2,
+            out_shape=shapes,
+            in_specs=[pl.BlockSpec(memory_space=pl.ANY)] * 5,
             out_specs=[vmem] * 4,
-            scratch_shapes=[block] * 4 + [
-                seg_block, seg_block,
+            scratch_shapes=[block] * 2 + [
+                pltpu.VMEM((1, rows), jnp.int32), seg_block, seg_block,
                 pltpu.VMEM((slots, HEADS, 2, rows), jnp.float32),
                 mask, mask,
-                dma((4,)), dma((4, 7, HEADS)), dma((4, slots + 1, HEADS)),
+                dma((5,)), dma((2, 7, HEADS)), dma((2, slots + 1, HEADS)),
                 dma((2, slots)), dma((2, slots)), dma((slots, HEADS)), dma((slots, HEADS)),
             ],
             compiler_params=pltpu.CompilerParams(
                 collective_id=0, has_side_effects=True, vmem_limit_bytes=VMEM_LIMIT
             ),
-        )(queries, keys, values, out_grad, seg_row, seg_col)
+        )(queries, keys, values, out_grad, segments[None, :])
+        return pl.pallas_call(
+            drain,
+            out_shape=shapes,
+            in_specs=[vmem] * 4,
+            out_specs=[pl.BlockSpec(memory_space=pl.ANY)] * 4,
+            scratch_shapes=[dma((4,))],
+            compiler_params=pltpu.CompilerParams(vmem_limit_bytes=DRAIN_LIMIT),
+        )(*results)
 
     rows_spec = P(("branch", "seq"), None)
     return jax.shard_map(

time: 105 us -> 98.2 us (0.935)
  local copies, waits for them, and re-layouts: 4.69 us -> 0.67 us
  Pallas kernels: 99.5 us -> 96.2 us
    pallas_call x1, Pallas kernels: 99.5 us -> 94.1 us  [local(): pl.pallas_call(functools.partial(kernel, count, rows, head_dim), out_shap...]
    unnamed x6 -> x2, local copies, waits for them, and re-layouts: 4.55 us -> 0.67 us
    pallas_call x0 -> x1, Pallas kernels: none -> 2.04 us  [local(): pl.pallas_call(drain, out_shape=shapes, in_specs=[vmem] * 4, out_specs=[p...]
where the time goes in v3:
time: 98.2 us; the launch traced here: 97.5 us
  Pallas kernels  96.2 us (98%)
    pallas_call x1, Pallas kernels, local(): pl.pallas_call(functools.partial(kernel, count, rows, head_dim), out_shap...  94.1 us
    pallas_call x1, Pallas kernels, local(): pl.pallas_call(drain, out_shape=shapes, in_specs=[vmem] * 4, out_specs=[p...  2.04 us

profile of v3, /device:TPU:7, one launch (start us, length us, event | category | flops | bytes accessed | tf_op | source)
XLA Modules:
  0.0 97.5 jit_solution(7183263708288298277)
XLA Ops:
  0.6 0.0 copy-start
  0.6 0.7 copy-done
  1.3 94.1 %shard_map.84 = (bf16[256,2048]{1,0:T(8,128)(2,1)S(1)}, bf16[256,2048]{1,0:T(8,128)(2,1)S(1)}, bf16[256,2048]{1,0:T(8,128)(2,1)S(1)}, bf16[256,2048]{1,0:T(8,128)(2,1)S(1)}) custom-call(bf16[256,2048]{1,0:T(8,128)(2,1)} %q_in.1, bf16[256,2048]{1,0:T(8,128)(2,1)} %k_in.1, bf16[256,2048]{1,0:T(8,128)(2,1)} %v_in.1, bf16[256,2048]{1,0:T(8,128)(2,1)} %g_in.1, ...), custom_call_target="tpu_custom_call" | custom-call | tf_op jit(solution)/shard_map/pallas_call | solution.py:431
  95.4 2.0 %shard_map.85 = (bf16[256,2048]{1,0:T(8,128)(2,1)}, bf16[256,2048]{1,0:T(8,128)(2,1)}, bf16[256,2048]{1,0:T(8,128)(2,1)}, bf16[256,2048]{1,0:T(8,128)(2,1)}) custom-call(bf16[256,2048]{1,0:T(8,128)(2,1)S(1)} %get-tuple-element.8.refs_0_, bf16[256,2048]{1,0:T(8,128)(2,1)S(1)} %get-tuple-element.9.refs_1_, bf16[256,2048]{1,0:T(8,128)(2,1)S(1)} %get-tuple-element.10.refs_2_, ...), custom_call_target="tpu_custom_call" | custom-call | tf_op jit(solution)/shard_map/pallas_call | solution.py:447
Async XLA Ops:
  0.6 0.7 copy-start

commit v4 on v3

--- a/solution.py
+++ b/solution.py
@@ -29,7 +29,7 @@
     q_in, k_in, v_in, g_in, seg_in,
     o_out, dq_out, dk_out, dv_out,
     kvb, qgb, seg_row, kseg, qseg, stat, bias, bias_t,
-    load_sem, send_sem, recv_sem, seg_send, seg_recv, stat_send, stat_recv,
+    load_sem, whole_sem, send_sem, recv_sem, seg_send, seg_recv, stat_send, stat_recv,
 ):
     me = lax.axis_index("seq")
     odd = me % 2
@@ -61,14 +61,20 @@
         pltpu.make_async_remote_copy(
             src_ref=piece(ts, from_slot, c),
             dst_ref=piece(ts, to_slot, c),
-            send_sem=send_sem.at[ts, kind, c],
-            recv_sem=recv_sem.at[ts, to_slot, c],
+            send_sem=whole_sem.at[ts, kind] if kind < 3 else send_sem.at[ts, c],
+            recv_sem=recv_sem.at[ts, to_slot - 1, c],
             device_id=to(target),
             device_id_type=MESH,
         ).start()
 
     def landed(ts, slot, c):
-        pltpu.make_async_copy(piece(ts, slot, c), piece(ts, slot, c), recv_sem.at[ts, slot, c]).wait()
+        pltpu.make_async_copy(piece(ts, slot, c), piece(ts, slot, c), recv_sem.at[ts, slot - 1, c]).wait()
+
+    def wait_many(part, sem, there):
+        for n in far:
+            @pl.when(there == n if n < REACH else there >= n)
+            def _():
+                pltpu.make_async_copy(part(n), part(n), sem).wait()
 
     direct_up = me + 1 + 2 * odd
     direct_down = me - 3 + 2 * odd
@@ -80,7 +86,7 @@
     above = pair + 1 < pairs
 
     def kv_near(row, c):
-        return c < chunks * (pairs - 1 - row) // pairs - 1
+        return c < chunks * (pairs - 1 - row) // pairs
 
     def qg_near(row, c):
         return c < (chunks - chunks // pairs) * row // pairs
@@ -116,7 +122,10 @@
     barrier = pltpu.get_barrier_semaphore()
     met = 0
     for d in (1, 2, 3, 4, 5):
-        for peer, there in ((me + d, me + d < count), (me - d, me - d >= 0)):
+        for peer, there in (
+            (me + d, (me + d < count) & ((d < 5) | (odd == 0))),
+            (me - d, (me - d >= 0) & ((d < 5) | (odd == 1))),
+        ):
             @pl.when(there)
             def _():
                 pl.semaphore_signal(barrier, inc=1, device_id=to(peer), device_id_type=MESH)
@@ -127,8 +136,8 @@
         return pltpu.make_async_remote_copy(
             src_ref=seg_row,
             dst_ref=(kseg, qseg)[way].at[d],
-            send_sem=seg_send.at[way, d],
-            recv_sem=seg_recv.at[way, d],
+            send_sem=seg_send.at[way],
+            recv_sem=seg_recv.at[way],
             device_id=to(target),
             device_id_type=MESH,
         )
@@ -242,14 +251,9 @@
     same = own_col == seg_row[0:1, :]
     bias[0] = jnp.where(same & (across <= upper), 0.0, HIDDEN)
     bias_t[0] = jnp.where(same & (upper <= across), 0.0, HIDDEN)
+    wait_many(lambda n: kseg.at[pl.ds(1, n)], seg_recv.at[0], me)
+    wait_many(lambda n: qseg.at[pl.ds(1, n)], seg_recv.at[1], count - 1 - me)
     for d in far:
-        @pl.when(me - d >= 0)
-        def _():
-            pltpu.make_async_copy(seg_row, kseg.at[d], seg_recv.at[0, d]).wait()
-
-        @pl.when(me + d < count)
-        def _():
-            pltpu.make_async_copy(seg_row, qseg.at[d], seg_recv.at[1, d]).wait()
         bias[d] = jnp.where(own_col == kseg[d, 0:1, :], 0.0, HIDDEN)
         bias_t[d] = jnp.where(own_col == qseg[d, 0:1, :], 0.0, HIDDEN)
     step_y(0)
@@ -310,8 +314,8 @@
                 pltpu.make_async_remote_copy(
                     src_ref=stat.at[0, c],
                     dst_ref=stat.at[d, c],
-                    send_sem=stat_send.at[d, c],
-                    recv_sem=stat_recv.at[d, c],
+                    send_sem=stat_send.at[d - 1],
+                    recv_sem=stat_recv.at[c],
                     device_id=to(me - d),
                     device_id_type=MESH,
                 ).start()
@@ -333,10 +337,7 @@
         @pl.when((me + 3 < count) & jnp.logical_not((odd == 1) & active(QG, 4, c)))
         def _():
             landed(QG, 3, c)
-        for d in far:
-            @pl.when(me + d < count)
-            def _():
-                pltpu.make_async_copy(stat.at[d, c], stat.at[d, c], stat_recv.at[d, c]).wait()
+        wait_many(lambda n: stat.at[pl.ds(1, n), c], stat_recv.at[c], count - 1 - me)
 
     def own_rest(c, carry):
         own_y(QG, c)
@@ -358,19 +359,15 @@
         send_stats(c)
         return carry
 
-    def sent(ts, c):
-        for kind in range(7):
-            @pl.when(active(ts, kind, c))
-            def _():
-                pltpu.make_async_copy(piece(ts, 0, c), piece(ts, 0, c), send_sem.at[ts, kind, c]).wait()
-
     def finish(c):
-        sent(KV, c)
-        sent(QG, c)
-        for d in far:
-            @pl.when(me - d >= 0)
-            def _():
-                pltpu.make_async_copy(stat.at[0, c], stat.at[0, c], stat_send.at[d, c]).wait()
+        for ts in (KV, QG):
+            own = active(ts, 3, c) | active(ts, 5, c) | active(ts, 6, c)
+            passed = active(ts, 4, c)
+            for slots, there in ((2, own & passed), (1, own != passed)):
+                @pl.when(there)
+                def _():
+                    part = bufs[ts].at[pl.ds(0, slots), :, :, columns(c)]
+                    pltpu.make_async_copy(part, part, send_sem.at[ts, c]).wait()
 
     def finish_rest(c, carry):
         finish(c)
@@ -396,14 +393,18 @@
     lax.fori_loop(0, chunks, key_step, 0)
 
     lax.fori_loop(chunks - LAG, chunks, finish_rest, 0)
+    for ts in (KV, QG):
+        for kind in range(3):
+            @pl.when(active(ts, kind, 0))
+            def _():
+                pltpu.make_async_copy(bufs[ts].at[0], bufs[ts].at[0], whole_sem.at[ts, kind]).wait()
     for d in far:
-        @pl.when(me + d < count)
-        def _():
-            pltpu.make_async_copy(seg_row, seg_row, seg_send.at[0, d]).wait()
-
         @pl.when(me - d >= 0)
         def _():
-            pltpu.make_async_copy(seg_row, seg_row, seg_send.at[1, d]).wait()
+            pltpu.make_async_copy(stat.at[0], stat.at[0], stat_send.at[d - 1]).wait()
+
+    wait_many(lambda n: kseg.at[pl.ds(1, n)], seg_send.at[0], count - 1 - me)
+    wait_many(lambda n: kseg.at[pl.ds(1, n)], seg_send.at[1], me)
 
 
 def drain(*refs):
@@ -437,8 +438,8 @@
                 pltpu.VMEM((1, rows), jnp.int32), seg_block, seg_block,
                 pltpu.VMEM((slots, HEADS, 2, rows), jnp.float32),
                 mask, mask,
-                dma((5,)), dma((2, 7, HEADS)), dma((2, slots + 1, HEADS)),
-                dma((2, slots)), dma((2, slots)), dma((slots, HEADS)), dma((slots, HEADS)),
+                dma((5,)), dma((2, 3)), dma((2, HEADS)), dma((2, slots, HEADS)),
+                dma((2,)), dma((2,)), dma((REACH,)), dma((HEADS,)),
             ],
             compiler_params=pltpu.CompilerParams(
                 collective_id=0, has_side_effects=True, vmem_limit_bytes=VMEM_LIMIT

time: 98.2 us -> 94.3 us (0.960)
  Pallas kernels: 96.2 us -> 92 us
    pallas_call x1, Pallas kernels: 94.1 us -> 89.9 us  [local(): pl.pallas_call(functools.partial(kernel, count, rows, head_dim), out_shap...]
where the time goes in v4:
time: 94.3 us; the launch traced here: 93.3 us
  Pallas kernels  92 us (98%)
    pallas_call x1, Pallas kernels, local(): pl.pallas_call(functools.partial(kernel, count, rows, head_dim), out_shap...  89.9 us
    pallas_call x1, Pallas kernels, local(): pl.pallas_call(drain, out_shape=shapes, in_specs=[vmem] * 4, out_specs=[p...  2.04 us

profile of v4, /device:TPU:7, one launch (start us, length us, event | category | flops | bytes accessed | tf_op | source)
XLA Modules:
  0.0 93.3 jit_solution(7174467458407056594)
XLA Ops:
  0.6 0.0 copy-start
  0.6 0.7 copy-done
  1.3 89.9 %shard_map.84 = (bf16[256,2048]{1,0:T(8,128)(2,1)S(1)}, bf16[256,2048]{1,0:T(8,128)(2,1)S(1)}, bf16[256,2048]{1,0:T(8,128)(2,1)S(1)}, bf16[256,2048]{1,0:T(8,128)(2,1)S(1)}) custom-call(bf16[256,2048]{1,0:T(8,128)(2,1)} %q_in.1, bf16[256,2048]{1,0:T(8,128)(2,1)} %k_in.1, bf16[256,2048]{1,0:T(8,128)(2,1)} %v_in.1, bf16[256,2048]{1,0:T(8,128)(2,1)} %g_in.1, ...), custom_call_target="tpu_custom_call" | custom-call | tf_op jit(solution)/shard_map/pallas_call | solution.py:432
  91.2 2.0 %shard_map.85 = (bf16[256,2048]{1,0:T(8,128)(2,1)}, bf16[256,2048]{1,0:T(8,128)(2,1)}, bf16[256,2048]{1,0:T(8,128)(2,1)}, bf16[256,2048]{1,0:T(8,128)(2,1)}) custom-call(bf16[256,2048]{1,0:T(8,128)(2,1)S(1)} %get-tuple-element.8.refs_0_, bf16[256,2048]{1,0:T(8,128)(2,1)S(1)} %get-tuple-element.9.refs_1_, bf16[256,2048]{1,0:T(8,128)(2,1)S(1)} %get-tuple-element.10.refs_2_, ...), custom_call_target="tpu_custom_call" | custom-call | tf_op jit(solution)/shard_map/pallas_call | solution.py:448
Async XLA Ops:
  0.6 0.7 copy-start

commit v5 on v4

--- a/solution.py
+++ b/solution.py
@@ -11,7 +11,7 @@
 HEADS = 16
 REACH = 3
 FILL = 6
-LAG = 4
+LAG = 2
 DRAIN_LIMIT = 48 * 1024 * 1024
 VMEM_LIMIT = 49 * 1024 * 1024
 MESH = pl.DeviceIdType.MESH
@@ -88,8 +88,11 @@
     def kv_near(row, c):
         return c < chunks * (pairs - 1 - row) // pairs
 
-    def qg_near(row, c):
-        return c < (chunks - chunks // pairs) * row // pairs
+    def qg_near(row, c, parity):
+        amount = (chunks - chunks // pairs) * row // pairs
+        early = chunks * 3 // 8
+        late = ((c - early) % 2 == 1) & (c < 2 * amount - early)
+        return (c < jnp.minimum(amount, early)) | ((c >= early) & late)
 
     paced = first & (odd == 1) & above & kv_near(pair, 0)
 
@@ -108,10 +111,10 @@
             last & (me - 2 >= 0),
             direct_down >= 0,
             me + 2 < count,
-            first & (odd == 1) & below & jnp.logical_not(qg_near(pair, c)),
-            first & above & jnp.logical_not(qg_near(pair + 1, c)),
-            first & below & qg_near(pair, c),
-            last & below & qg_near(pair, c),
+            first & (odd == 1) & below & jnp.logical_not(qg_near(pair, c, odd)),
+            first & above & jnp.logical_not(qg_near(pair + 1, c, 1 - odd)),
+            first & below & qg_near(pair, c, odd),
+            last & below & qg_near(pair, c, odd),
         )[kind]
 
     loads = [pltpu.make_async_copy(ins[t], bufs[t // 2].at[0, t % 2], load_sem.at[t]) for t in range(4)]

time: 94.3 us -> 93.4 us (level)
  no operation moved by 1% of the time
where the time goes in v5:
time: 93.4 us; the launch traced here: 93.2 us
  Pallas kernels  91.9 us (98%)
    pallas_call x1, Pallas kernels, local(): pl.pallas_call(functools.partial(kernel, count, rows, head_dim), out_shap...  89.9 us
    pallas_call x1, Pallas kernels, local(): pl.pallas_call(drain, out_shape=shapes, in_specs=[vmem] * 4, out_specs=[p...  2.04 us

profile of v5, /device:TPU:7, one launch (start us, length us, event | category | flops | bytes accessed | tf_op | source)
XLA Modules:
  0.0 93.2 jit_solution(16807187373311045379)
XLA Ops:
  0.6 0.0 copy-start
  0.6 0.7 copy-done
  1.3 89.9 %shard_map.84 = (bf16[256,2048]{1,0:T(8,128)(2,1)S(1)}, bf16[256,2048]{1,0:T(8,128)(2,1)S(1)}, bf16[256,2048]{1,0:T(8,128)(2,1)S(1)}, bf16[256,2048]{1,0:T(8,128)(2,1)S(1)}) custom-call(bf16[256,2048]{1,0:T(8,128)(2,1)} %q_in.1, bf16[256,2048]{1,0:T(8,128)(2,1)} %k_in.1, bf16[256,2048]{1,0:T(8,128)(2,1)} %v_in.1, bf16[256,2048]{1,0:T(8,128)(2,1)} %g_in.1, ...), custom_call_target="tpu_custom_call" | custom-call | tf_op jit(solution)/shard_map/pallas_call | solution.py:435
  91.2 2.0 %shard_map.85 = (bf16[256,2048]{1,0:T(8,128)(2,1)}, bf16[256,2048]{1,0:T(8,128)(2,1)}, bf16[256,2048]{1,0:T(8,128)(2,1)}, bf16[256,2048]{1,0:T(8,128)(2,1)}) custom-call(bf16[256,2048]{1,0:T(8,128)(2,1)S(1)} %get-tuple-element.8.refs_0_, bf16[256,2048]{1,0:T(8,128)(2,1)S(1)} %get-tuple-element.9.refs_1_, bf16[256,2048]{1,0:T(8,128)(2,1)S(1)} %get-tuple-element.10.refs_2_, ...), custom_call_target="tpu_custom_call" | custom-call | tf_op jit(solution)/shard_map/pallas_call | solution.py:451
Async XLA Ops:
  0.6 0.7 copy-start
